TPU v7x, 512 devices: a whole 4x8x8 slice. The times are simulated.
512 devices in a mesh: depth: 256 (over z, y, x), chan: 2 (over core).
Axes of the slice: x: 4, y: 8, z: 8, core: 2. Of those that a mesh axis runs over, the one named last changes fastest.
Arguments:
- feats: bfloat16 [32, 512, 8, 128], P('chan', 'depth'), may hold values from -6 to 6
- weight_one: bfloat16 [32, 32, 27], replicated, may hold values from -0.21875 to 0.21875
- weight_two: bfloat16 [64, 32, 27], replicated, may hold values from -0.21875 to 0.21875
- cotangent: bfloat16 [64, 256, 4, 64], P('chan', 'depth'), may hold values from -6 to 6
Outputs:
- grad_feats: bfloat16 [32, 512, 8, 128], P('chan', 'depth')
- grad_weight_one: float32 [32, 32, 27], P(None, 'chan')
- grad_weight_two: float32 [64, 32, 27], P(None, 'chan')
All inputs are finite; a program needn't handle non-finite values.
Results may differ from a plain program's by a relative error of at most 0.013.
Values may be sent and summed in bfloat16 or wider, within the bound.
A program may use at most 128 MiB of HBM per device.

v0:
```python
import functools

import jax
import jax.numpy as jnp
from jax import lax
from jax.sharding import Mesh
from jax.sharding import PartitionSpec as P

DEPTH = ("depth_0", "depth_1", "depth_2")


OFFSETS = [
    (first, second, third) for first in range(3) for second in range(3) for third in range(3)
]


def padded_2(block, sides, width):
    for axis, dim in sides:
        count = lax.axis_size(axis)
        forward = [(i, i + 1) for i in range(count - 1)]
        backward = [(target, source) for source, target in forward]
        low = lax.ppermute(
            lax.slice_in_dim(block, block.shape[dim] - width, None, axis=dim), axis, forward
        )
        high = lax.ppermute(lax.slice_in_dim(block, 0, width, axis=dim), axis, backward)
        block = jnp.concatenate([low, block, high], axis=dim)
    return block


def split_up(x, dim, count):
    before, after = (x.shape[:dim], x.shape[dim + 1 :])
    return jnp.moveaxis(x.reshape(*before, count, -1, *after), dim, 0)


def summed_on_arrival(x, axis, dim):
    count = lax.axis_size(axis)
    pieces = lax.all_to_all(split_up(x, dim, count), axis, 0, 0, tiled=True)
    return jnp.sum(pieces.astype(jnp.float32), axis=0)


def joined_along(pieces, dim):
    pieces = jnp.moveaxis(pieces, 0, dim)
    shape = pieces.shape
    return pieces.reshape(*shape[:dim], shape[dim] * shape[dim + 1], *shape[dim + 2 :])


def from_everyone(x, axis):
    copies = jnp.broadcast_to(x, (lax.axis_size(axis), *x.shape))
    return lax.all_to_all(copies, axis, split_axis=0, concat_axis=0, tiled=True)


def gather_directly(x, axis, dim):
    return joined_along(from_everyone(x, axis), dim)


def one_axis_at_a_time(x, axes):
    return functools.reduce(lax.psum, axes, x)


def pad_plane(haloed):
    return jnp.pad(haloed, ((0, 0), (0, 0), (1, 1), (1, 1)))


def cut_edges(haloed, lower_keep, upper_keep):
    count = haloed.shape[1]
    position = lax.iota(jnp.int32, count)
    keep = jnp.where(position == 0, lower_keep, jnp.where(position == count - 1, upper_keep, True))
    return jnp.where(keep[None, :, None, None], haloed, jnp.zeros((), haloed.dtype))


def patch_rows(haloed):
    chans = haloed.shape[0]
    planes = haloed.shape[1] - 2
    height = haloed.shape[2]
    across = haloed.shape[3]
    padded = pad_plane(haloed)
    windows = [
        padded[:, first : first + planes, second : second + height, third : third + across]
        for first, second, third in OFFSETS
    ]
    return jnp.stack(windows, 0).reshape(27 * chans, planes * height * across)


def flat_weight(own):
    return jnp.transpose(own, (0, 2, 1)).reshape(own.shape[0], -1)


def flat_transposed(own):
    return jnp.transpose(own, (2, 1, 0)).reshape(-1, own.shape[0])


def weight_layout(weight_sum, chans):
    return jnp.transpose(weight_sum.reshape(weight_sum.shape[0], 27, chans), (0, 2, 1))


def slope(pre):
    sig = jax.nn.sigmoid(pre)
    return sig * (1.0 + pre * (1.0 - sig))


def grad_fold(transposed, patches, piece):
    count = piece.shape[0]
    padded = pad_plane(piece).reshape(count, -1)
    image_sum = jnp.dot(transposed, padded, preferred_element_type=jnp.float32)
    inner = piece[:, 1:-1].reshape(count, -1)
    rows_part = lax.dot_general(
        inner, patches, (((1,), (1,)), ((), ())), preferred_element_type=jnp.float32
    )
    return (image_sum, rows_part)


def shift_sum(image_sum, chans, planes, height, across):
    shaped = image_sum.reshape(27, chans, planes + 2, height + 2, across + 2)
    total = jnp.zeros((chans, planes, height, across), jnp.float32)
    for index, (first, second, third) in enumerate(OFFSETS):
        total = (
            total
            + shaped[
                index,
                :,
                2 - first : 2 - first + planes,
                2 - second : 2 - second + height,
                2 - third : 2 - third + across,
            ]
        )
    return total


def shards(feats, weight_one, weight_two, cotangent):
    groups = lax.axis_size("chan")
    member = lax.axis_index("chan")
    slabs = lax.axis_size(DEPTH)
    place = lax.axis_index(DEPTH)
    lower_keep = place % slabs != 0
    upper_keep = (place + 1) % slabs != 0
    in_chans, planes, height, across = feats.shape
    mid_chans = weight_one.shape[0] // groups
    out_chans = weight_two.shape[0] // groups
    feats_halo = cut_edges(padded_2(feats, ((DEPTH, 1),), 1), lower_keep, upper_keep)
    patches_one = patch_rows(feats_halo)
    own_one = lax.dynamic_slice_in_dim(weight_one, member * in_chans, in_chans, 1)
    partial_one = jnp.dot(flat_weight(own_one), patches_one, preferred_element_type=jnp.float32)
    pre_one = summed_on_arrival(partial_one.astype(jnp.bfloat16), "chan", 0)
    act_one = jax.nn.silu(pre_one).astype(jnp.bfloat16).reshape(mid_chans, planes, height, across)
    pooled = (
        act_one.astype(jnp.float32)
        .reshape(mid_chans, planes // 2, 2, height // 2, 2, across // 2, 2)
        .mean(axis=(2, 4, 6))
        .astype(jnp.bfloat16)
    )
    pooled_halo = cut_edges(padded_2(pooled, ((DEPTH, 1),), 1), lower_keep, upper_keep)
    patches_two = patch_rows(pooled_halo)
    own_two = lax.dynamic_slice_in_dim(weight_two, member * mid_chans, mid_chans, 1)
    partial_two = jnp.dot(flat_weight(own_two), patches_two, preferred_element_type=jnp.float32)
    pre_two = summed_on_arrival(partial_two.astype(jnp.bfloat16), "chan", 0)
    grad_two = (cotangent.astype(jnp.float32).reshape(out_chans, -1) * slope(pre_two)).astype(
        jnp.bfloat16
    )
    grad_two = grad_two.reshape(out_chans, planes // 2, height // 2, across // 2)
    grad_two_halo = cut_edges(padded_2(grad_two, ((DEPTH, 1),), 1), lower_keep, upper_keep)
    image_two, wsum_two = grad_fold(
        flat_transposed(own_two), patches_two, gather_directly(grad_two_halo, "chan", 0)
    )
    grad_weight_two = weight_layout(wsum_two, mid_chans)
    grad_weight_two = one_axis_at_a_time(grad_weight_two, DEPTH)
    back_pooled = shift_sum(image_two, mid_chans, planes // 2, height // 2, across // 2)
    spread = (
        jnp.broadcast_to(
            back_pooled[:, :, None, :, None, :, None],
            (mid_chans, planes // 2, 2, height // 2, 2, across // 2, 2),
        ).reshape(mid_chans, -1)
        * 0.125
    )
    grad_one = (
        (spread * slope(pre_one)).astype(jnp.bfloat16).reshape(mid_chans, planes, height, across)
    )
    grad_one_halo = cut_edges(padded_2(grad_one, ((DEPTH, 1),), 1), lower_keep, upper_keep)
    image_one, wsum_one = grad_fold(
        flat_transposed(own_one), patches_one, gather_directly(grad_one_halo, "chan", 0)
    )
    grad_weight_one = weight_layout(wsum_one, in_chans)
    grad_weight_one = one_axis_at_a_time(grad_weight_one, DEPTH)
    grad_feats = shift_sum(image_one, in_chans, planes, height, across).astype(jnp.bfloat16)
    return (grad_feats, grad_weight_one, grad_weight_two)


def solution(mesh):
    finer = Mesh(
        mesh.devices.reshape(8, 8, 4, mesh.shape["chan"]), ("depth_0", "depth_1", "depth_2", "chan")
    )
    in_specs = (P("chan", DEPTH, None, None), P(), P(), P("chan", DEPTH, None, None))
    out_specs = (P("chan", DEPTH, None, None), P(None, "chan", None), P(None, "chan", None))
    return jax.shard_map(
        shards, mesh=finer, in_specs=in_specs, out_specs=out_specs, check_vma=False
    )
```

profile of v0, /device:TPU:1, one launch (start us, length us, event | category | flops | bytes accessed | tf_op | source)
XLA Modules:
  0.0 343.1 jit_solution(2406383492196253577)
XLA Ops:
  7.2 0.8 fusion.81
  8.1 3.9 %collective-permute-start = (bf16[16,1,8,128]{3,2,1,0:T(8,128)(2,1)S(1)}, bf16[16,1,8,128]{3,2,1,0:T(8,128)(2,1)S(1)}, u32[]{:S(2)}, u32[]{:S(2)}) collective-permute-start(bf16[16,1,8,128]{3,2,1,0:T(8,128)(2,1)S(1)} %get-tuple-element.149), channel_id=1, source_target_pairs={{0,2},{2,4},{4,6},{6,8},{8,10},{10,12},{12,14},{14,16},{16,18},{18... | collective-permute-start | bytes 98312 | tf_op jit(solution)/shard_map/ppermute | solution.py:22
  12.0 1.3 collective-permute-start.1
  14.0 1.1 constant_dynamic-slice_fusion.1
  15.2 1.4 collective-permute-done.1
  16.6 0.9 maximum_select_fusion
  19.7 0.8 copy.2480
  20.5 0.8 copy.2481
  22.7 0.8 copy.2485
  28.7 0.8 copy.2494
  30.9 0.8 copy.2497
  33.2 10.8 %stack.195 = bf16[27,16,2,8,128]{4,0,3,1,2:T(8,128)(2,1)S(1)} concatenate(bf16[1,16,2,8,128]{4,0,3,1,2:T(2,128)(2,1)S(1)} %copy.2479, bf16[1,16,2,8,128]{4,0,3,1,2:T(2,128)(2,1)} %copy.2480, bf16[1,16,2,8,128]{4,0,3,1,2:T(2,128)(2,1)} %copy.2481, bf16[1,16,2,8,128]{4,0,3,1,2:T(2,128)(2,1)} %copy.2482, bf16[1,16,2,8,128]{4,0,3,1,2:T(2,128)(2,1)S(1)} %copy.2483, ...), dimensions={0} | concatenate | bytes 3538944 | tf_op jit(solution)/shard_map/stack | solution.py:81
  44.0 1.9 copy.2506
  46.0 3.8 %reshape.401 = bf16[432,2048]{1,0:T(8,128)(2,1)} reshape(bf16[27,16,2,8,128]{4,3,2,1,0:T(8,128)(2,1)} %copy.2506) | data formatting | bytes 3538944 | tf_op jit(solution)/shard_map/reshape | solution.py:81
  49.8 1.9 convolution_convert_fusion
  51.7 8.8 %all_to_all.20 = bf16[2,16,2048]{2,1,0:T(8,128)(2,1)S(1)} all-to-all(bf16[2,16,2048]{2,1,0:T(8,128)(2,1)S(1)} %bitcast.385), channel_id=1, replica_groups=mesh['depth_0'=8,'depth_1'=8,'depth_2'=4,'chan'=2] {'chan'}, dimensions={0} | all-to-all | bytes 262144 | tf_op jit(solution)/shard_map/all_to_all | solution.py:37
  60.9 1.1 copy.2509
  62.0 1.1 convert_reduce_fusion
  63.1 1.3 collective-permute-start.3
  64.4 4.0 %collective-permute-start.2 = (bf16[16,1,4,64]{3,2,0,1:T(4,128)(2,1)S(1)}, bf16[16,1,4,64]{3,2,0,1:T(4,128)(2,1)S(1)}, u32[]{:S(2)}, u32[]{:S(2)}) collective-permute-start(bf16[16,1,4,64]{3,2,0,1:T(4,128)(2,1)S(1)} %bitcast.415), channel_id=1, source_target_pairs={{0,2},{2,4},{4,6},{6,8},{8,10},{10,12},{12,14},{14,16},{16,18},{18... | collective-permute-start | bytes 24584 | tf_op jit(solution)/shard_map/ppermute | solution.py:22
  68.4 0.8 collective-permute-done.2
  71.8 4.9 %all_to_all.21 = bf16[2,32,256]{2,1,0:T(8,128)(2,1)S(1)} all-to-all(bf16[2,32,256]{2,1,0:T(8,128)(2,1)S(1)} %bitcast.413), channel_id=1, replica_groups=mesh['depth_0'=8,'depth_1'=8,'depth_2'=4,'chan'=2] {'chan'}, dimensions={0} | all-to-all | bytes 65536 | tf_op jit(solution)/shard_map/all_to_all | solution.py:37
  76.9 1.3 collective-permute-start.5
  78.2 4.5 %collective-permute-start.4 = (bf16[32,1,4,64]{3,2,1,0:T(4,128)(2,1)S(1)}, bf16[32,1,4,64]{3,2,1,0:T(4,128)(2,1)S(1)}, u32[]{:S(2)}, u32[]{:S(2)}) collective-permute-start(bf16[32,1,4,64]{3,2,1,0:T(4,128)(2,1)S(1)} %multiply_convert_fusion.2), channel_id=1, source_target_pairs={{0,2},{2,4},{4,6},{6,8},{8,10},{10,12},{12,14},{14,16},{16,18},{18... | collective-permute-start | bytes 49160 | tf_op jit(solution)/shard_map/ppermute | solution.py:22
  84.2 4.7 %all_to_all.22 = bf16[2,2,12288]{2,1,0:T(2,128)(2,1)S(1)} all-to-all(bf16[2,2,12288]{2,1,0:T(2,128)(2,1)S(1)} %reshape.443), channel_id=1, replica_groups=mesh['depth_0'=8,'depth_1'=8,'depth_2'=4,'chan'=2] {'chan'}, dimensions={0} | all-to-all | bytes 196608 | tf_op jit(solution)/shard_map/all_to_all | solution.py:49
  89.5 0.9 reshape.406
  90.4 1.3 dot_general.29
  92.8 1.0 fusion.78
  94.0 0.8 copy.2542
  94.7 1.0 broadcast_in_dim.101
  95.9 1.0 multiply_convert_fusion.1
  96.9 3.9 %collective-permute-start.6 = (bf16[16,1,8,128]{3,2,1,0:T(8,128)(2,1)S(1)}, bf16[16,1,8,128]{3,2,1,0:T(8,128)(2,1)S(1)}, u32[]{:S(2)}, u32[]{:S(2)}) collective-permute-start(bf16[16,1,8,128]{3,2,1,0:T(8,128)(2,1)S(1)} %get-tuple-element.147), channel_id=1, source_target_pairs={{0,2},{2,4},{4,6},{6,8},{8,10},{10,12},{12,14},{14,16},{16,18},{18... | collective-permute-start | bytes 98312 | tf_op jit(solution)/shard_map/ppermute | solution.py:22
  100.9 1.3 collective-permute-start.7
  102.2 1.1 convolution_bitcast_fusion
  103.3 2.5 collective-permute-done.7
  106.0 5.0 %all_to_all.23 = bf16[2,16,4,8,128]{4,1,3,2,0:T(8,128)(2,1)S(1)} all-to-all(bf16[2,16,4,8,128]{4,1,3,2,0:T(8,128)(2,1)S(1)} %broadcast_in_dim.103), channel_id=1, replica_groups=mesh['depth_0'=8,'depth_1'=8,'depth_2'=4,'chan'=2] {'chan'}, dimensions={0} | all-to-all | bytes 524288 | tf_op jit(solution)/shard_map/all_to_all | solution.py:49
  112.5 1.6 reshape.408
  114.1 2.8 dot_general.32
  117.0 2.5 fusion
  120.1 79.2 %all-reduce.8.cloned.1.call-done = f32[64,16,27]{0,2,1:T(8,128)} async-done(((f32[64,16,27]{0,2,1:T(8,128)}), f32[64,16,27]{0,2,1:T(8,128)}) %all-reduce.8.cloned.1.call-update) | async-done | bytes 110608 | tf_op jit(solution)/shard_map/psum | solution.py:57
  199.4 1.7 convolution_bitcast_fusion.1
  201.1 25.6 %psum.42 = f32[32,16,27]{2,0,1:T(8,128)S(1)} all-reduce(f32[32,16,27]{2,0,1:T(8,128)S(1)} %convolution_bitcast_fusion.1), channel_id=1, replica_groups=mesh['depth_0'=8,'depth_1'=8,'depth_2'=4,'chan'=2] {'depth_0'}, use_global_device_ids=true, to_apply=%region_3.4 | all-reduce | flops 13824 | bytes 110592 | tf_op jit(solution)/shard_map/psum | solution.py:57
  226.7 51.0 %all-reduce.10.cloned.1.call-done = f32[64,16,27]{0,2,1:T(8,128)} async-done(((f32[64,16,27]{0,2,1:T(8,128)}), f32[64,16,27]{0,2,1:T(8,128)}) %all-reduce.10.cloned.1.call-update) | async-done | bytes 110608 | tf_op jit(solution)/shard_map/psum | solution.py:57
  277.7 25.7 %psum.43 = f32[32,16,27]{2,0,1:T(8,128)S(1)} all-reduce(f32[32,16,27]{2,0,1:T(8,128)S(1)} %psum.42), channel_id=1, replica_groups=mesh['depth_0'=8,'depth_1'=8,'depth_2'=4,'chan'=2] {'depth_1'}, use_global_device_ids=true, to_apply=%region_4.5 | all-reduce | flops 13824 | bytes 110592 | tf_op jit(solution)/shard_map/psum | solution.py:57
  303.4 15.9 %psum.44 = f32[32,16,27]{2,0,1:T(8,128)S(1)} all-reduce(f32[32,16,27]{2,0,1:T(8,128)S(1)} %psum.43), channel_id=1, replica_groups=mesh['depth_0'=8,'depth_1'=8,'depth_2'=4,'chan'=2] {'depth_2'}, use_global_device_ids=true, to_apply=%region_5.6 | all-reduce | flops 13824 | bytes 110592 | tf_op jit(solution)/shard_map/psum | solution.py:57
  319.3 0.9 copy.2550
  320.8 14.0 %all-reduce.12.cloned.1.call-done = f32[64,16,27]{0,2,1:T(8,128)} async-done(((f32[64,16,27]{0,2,1:T(8,128)}), f32[64,16,27]{0,2,1:T(8,128)}) %all-reduce.12.cloned.1.call-update) | async-done | bytes 110608 | tf_op jit(solution)/shard_map/psum | solution.py:57
  334.8 1.8 copy.2551
  (112 shorter events, 22.1 us)
Async XLA Ops:
  7.2 6.2 %copy-start = (bf16[64,32,27]{0,1,2:T(8,128)(2,1)S(1)}, bf16[64,32,27]{0,1,2:T(8,128)(2,1)}, u32[]{:S(2)}) copy-start(bf16[64,32,27]{0,1,2:T(8,128)(2,1)} %param.6) | copy-start | bytes 331780
  7.2 192.2 %all-reduce.8.cloned.1.call-start = ((), (), s32[]{:S(2)}) async-start(), calls=%async_computation.4 | async-start | bytes 524288 | tf_op jit(solution)/shard_map/psum | solution.py:57
  8.1 7.2 %collective-permute-start = (bf16[16,1,8,128]{3,2,1,0:T(8,128)(2,1)S(1)}, bf16[16,1,8,128]{3,2,1,0:T(8,128)(2,1)S(1)}, u32[]{:S(2)}, u32[]{:S(2)}) collective-permute-start(bf16[16,1,8,128]{3,2,1,0:T(8,128)(2,1)S(1)} %get-tuple-element.149), channel_id=1, source_target_pairs={{0,2},{2,4},{4,6},{6,8},{8,10},{10,12},{12,14},{14,16},{16,18},{18... | collective-permute-start | bytes 98312 | tf_op jit(solution)/shard_map/ppermute | solution.py:22
  12.0 4.7 %collective-permute-start.1 = (bf16[16,1,8,128]{3,2,1,0:T(8,128)(2,1)S(1)}, bf16[16,1,8,128]{3,2,1,0:T(8,128)(2,1)S(1)}, u32[]{:S(2)}, u32[]{:S(2)}) collective-permute-start(bf16[16,1,8,128]{3,2,1,0:T(8,128)(2,1)S(1)} %get-tuple-element.150), channel_id=1, source_target_pairs={{2,0},{4,2},{6,4},{8,6},{10,8},{12,10},{14,12},{16,14},{18,16},{20... | collective-permute-start | bytes 98312 | tf_op jit(solution)/shard_map/ppermute | solution.py:25
  15.2 34.6 %copy-start.4 = (bf16[32,16,27]{0,1,2:T(8,128)(2,1)}, bf16[32,16,27]{0,1,2:T(8,128)(2,1)S(1)}, u32[]{:S(2)}) copy-start(bf16[32,16,27]{0,1,2:T(8,128)(2,1)S(1)} %copy.2558) | copy-start | bytes 82948
  60.9 15.9 %copy-start.6 = (bf16[32,1,4,64]{3,2,1,0:T(4,128)(2,1)S(1)}, bf16[32,1,4,64]{3,2,1,0:T(4,128)(2,1)}, u32[]{:S(2)}) copy-start(bf16[32,1,4,64]{3,2,1,0:T(4,128)(2,1)} %param.7) | copy-start | bytes 49156
  62.0 9.6 %copy-start.3 = (bf16[64,16,27]{0,1,2:T(8,128)(2,1)S(1)}, bf16[64,16,27]{0,1,2:T(8,128)(2,1)}, u32[]{:S(2)}) copy-start(bf16[64,16,27]{0,1,2:T(8,128)(2,1)} %constant_dynamic-slice_fusion) | copy-start | bytes 165892
  63.1 5.3 %collective-permute-start.3 = (bf16[16,1,4,64]{3,2,0,1:T(4,128)(2,1)S(1)}, bf16[16,1,4,64]{3,2,0,1:T(4,128)(2,1)S(1)}, u32[]{:S(2)}, u32[]{:S(2)}) collective-permute-start(bf16[16,1,4,64]{3,2,0,1:T(4,128)(2,1)S(1)} %bitcast.414), channel_id=1, source_target_pairs={{2,0},{4,2},{6,4},{8,6},{10,8},{12,10},{14,12},{16,14},{18,16},{20... | collective-permute-start | bytes 24584 | tf_op jit(solution)/shard_map/ppermute | solution.py:25
  64.4 4.8 %collective-permute-start.2 = (bf16[16,1,4,64]{3,2,0,1:T(4,128)(2,1)S(1)}, bf16[16,1,4,64]{3,2,0,1:T(4,128)(2,1)S(1)}, u32[]{:S(2)}, u32[]{:S(2)}) collective-permute-start(bf16[16,1,4,64]{3,2,0,1:T(4,128)(2,1)S(1)} %bitcast.415), channel_id=1, source_target_pairs={{0,2},{2,4},{4,6},{6,8},{8,10},{10,12},{12,14},{14,16},{16,18},{18... | collective-permute-start | bytes 24584 | tf_op jit(solution)/shard_map/ppermute | solution.py:22
  76.9 6.5 %collective-permute-start.5 = (bf16[32,1,4,64]{3,2,1,0:T(4,128)(2,1)S(1)}, bf16[32,1,4,64]{3,2,1,0:T(4,128)(2,1)S(1)}, u32[]{:S(2)}, u32[]{:S(2)}) collective-permute-start(bf16[32,1,4,64]{3,2,1,0:T(4,128)(2,1)S(1)} %multiply_convert_fusion.2), channel_id=1, source_target_pairs={{2,0},{4,2},{6,4},{8,6},{10,8},{12,10},{14,12},{16,14},{18,16},{20... | collective-permute-start | bytes 49160 | tf_op jit(solution)/shard_map/ppermute | solution.py:25
  78.2 5.6 %collective-permute-start.4 = (bf16[32,1,4,64]{3,2,1,0:T(4,128)(2,1)S(1)}, bf16[32,1,4,64]{3,2,1,0:T(4,128)(2,1)S(1)}, u32[]{:S(2)}, u32[]{:S(2)}) collective-permute-start(bf16[32,1,4,64]{3,2,1,0:T(4,128)(2,1)S(1)} %multiply_convert_fusion.2), channel_id=1, source_target_pairs={{0,2},{2,4},{4,6},{6,8},{8,10},{10,12},{12,14},{14,16},{16,18},{18... | collective-permute-start | bytes 49160 | tf_op jit(solution)/shard_map/ppermute | solution.py:22
  96.9 6.4 %collective-permute-start.6 = (bf16[16,1,8,128]{3,2,1,0:T(8,128)(2,1)S(1)}, bf16[16,1,8,128]{3,2,1,0:T(8,128)(2,1)S(1)}, u32[]{:S(2)}, u32[]{:S(2)}) collective-permute-start(bf16[16,1,8,128]{3,2,1,0:T(8,128)(2,1)S(1)} %get-tuple-element.147), channel_id=1, source_target_pairs={{0,2},{2,4},{4,6},{6,8},{8,10},{10,12},{12,14},{14,16},{16,18},{18... | collective-permute-start | bytes 98312 | tf_op jit(solution)/shard_map/ppermute | solution.py:22
  100.9 4.9 %collective-permute-start.7 = (bf16[16,1,8,128]{3,2,1,0:T(8,128)(2,1)S(1)}, bf16[16,1,8,128]{3,2,1,0:T(8,128)(2,1)S(1)}, u32[]{:S(2)}, u32[]{:S(2)}) collective-permute-start(bf16[16,1,8,128]{3,2,1,0:T(8,128)(2,1)S(1)} %get-tuple-element.148), channel_id=1, source_target_pairs={{2,0},{4,2},{6,4},{8,6},{10,8},{12,10},{14,12},{16,14},{18,16},{20... | collective-permute-start | bytes 98312 | tf_op jit(solution)/shard_map/ppermute | solution.py:25
  103.3 174.4 %all-reduce.10.cloned.1.call-start = ((), (), s32[]{:S(2)}) async-start(), calls=%async_computation.5 | async-start | bytes 524288 | tf_op jit(solution)/shard_map/psum | solution.py:57
  111.1 0.7 copy-start.1
  111.9 5.1 %copy-start.5 = (bf16[32,16,27]{0,1,2:T(8,128)(2,1)S(1)}, bf16[32,16,27]{0,1,2:T(8,128)(2,1)}, u32[]{:S(2)}) copy-start(bf16[32,16,27]{0,1,2:T(8,128)(2,1)} %copy-done.4) | copy-start | bytes 82948
  119.4 80.0 %copy-start.2 = (bf16[2,16,4,8,128]{4,1,0,3,2:T(8,128)(2,1)S(1)}, bf16[2,16,4,8,128]{4,1,0,3,2:T(8,128)(2,1)}, u32[]{:S(2)}) copy-start(bf16[2,16,4,8,128]{4,1,0,3,2:T(8,128)(2,1)} %copy-done.1) | copy-start | bytes 786436
  199.4 135.5 %all-reduce.12.cloned.1.call-start = ((), (), s32[]{:S(2)}) async-start(), calls=%async_computation.6 | async-start | bytes 524288 | tf_op jit(solution)/shard_map/psum | solution.py:57
Sparse Core Ops, SparseCore 0:
  103.4 95.8 all-reduce.7
  201.6 76.0 all-reduce.9
  280.0 54.7 all-reduce.11
where the time goes:
time: 346 us; the launch traced here: 343 us
  waiting for transfers between devices  149 us (43%)
  blocking collectives  90.6 us (26%)
  local copies, waits for them, and re-layouts  55 us (16%)
  starting transfers between devices  21.7 us (6%)
  between operations  14.3 us (4%)
  matrix products  8.1 us (2%)
  other arithmetic  4.15 us (1%)
    psum x3, waiting for transfers between devices, one_axis_at_a_time(): return functools.reduce(lax.psum, axes, x)  144 us
    psum x3, blocking collectives, one_axis_at_a_time(): return functools.reduce(lax.psum, axes, x)  67.1 us
    another operation x32, local copies, waits for them, and re-layouts, patch_rows(): return jnp.stack(windows, 0).reshape(27 * chans, planes * height * across)  28.4 us
    ppermute x4, starting transfers between devices, padded_2(): lax.ppermute(lax.slice_in_dim(block, block.shape[dim] - width, None, axis...  16.4 us
    all_to_all x2, blocking collectives, summed_on_arrival(): pieces = lax.all_to_all(split_up(x, dim, count), axis, 0, 0, tiled=True)  13.7 us
    all_to_all x2, blocking collectives, from_everyone(): return lax.all_to_all(copies, axis, split_axis=0, concat_axis=0, tiled=True)  9.73 us
    unnamed x51, local copies, waits for them, and re-layouts  7.37 us
  transfers between devices with their start and end apart: 11, of which 7 were waited for; matrix products, arithmetic and copies ran while one was open for 4% of the time, Pallas kernels for 0%

commit v1 on v0

v1 whole, which is shorter than its diff:
```python
import functools

import jax
import jax.numpy as jnp
from jax import lax
from jax.experimental import pallas as pl
from jax.experimental.pallas import tpu as pltpu
from jax.sharding import Mesh
from jax.sharding import PartitionSpec as P

MESH = pl.DeviceIdType.MESH
F32 = jnp.float32
BF16 = jnp.bfloat16
AXES = ("z", "y", "x", "core")
ROWS = 512


def slope_of(pre, sig):
    return sig * (1.0 + pre * (1.0 - sig))


def fill_columns(dst, plane, chans, row, value, edges):
    lane = lax.broadcasted_iota(jnp.int32, value.shape, 1)
    left = pltpu.roll(value, 1, 1)
    right = pltpu.roll(value, 127, 1)
    if edges:
        left = jnp.where(lane == 0, 0.0, left)
        right = jnp.where(lane == 127, 0.0, right)
    where = slice((row + 1) * 128, (row + 2) * 128)
    dst[plane, 0:chans, where] = left.astype(BF16)
    dst[plane, chans : 2 * chans, where] = value.astype(BF16)
    dst[plane, 2 * chans : 3 * chans, where] = right.astype(BF16)


def clear_rows(dst, rows):
    planes, chans = dst.shape[:2]
    zero = jnp.zeros((planes, chans, 128), BF16)
    dst[:, :, 0:128] = zero
    dst[:, :, (rows + 1) * 128 : (rows + 2) * 128] = zero


def windows(src, planes, width):
    pieces = [src[a, :, b * 128 : b * 128 + width] for a in planes for b in range(3)]
    return jnp.concatenate(pieces, axis=0)


def own_windows(src, planes, width, core):
    pieces = []
    for a in planes:
        for b in range(3):
            for c in range(3):
                first = pl.multiple_of(c * 32 + core * 16, 16)
                pieces.append(src[a, pl.ds(first, 16), b * 128 : b * 128 + width])
    return jnp.concatenate(pieces, axis=0)


def pack_rows(rows):
    return jnp.concatenate(
        [rows[0] + pltpu.roll(rows[2], 64, 1), rows[1] + pltpu.roll(rows[3], 64, 1)], axis=1
    )


def unpack_into(dst, plane, chans, packed):
    lane = lax.broadcasted_iota(jnp.int32, (chans, 128), 1)
    for j in range(2):
        both = packed[:, j * 128 : (j + 1) * 128]
        low = jnp.where(lane < 64, both, 0.0)
        high = jnp.where(lane < 64, pltpu.roll(both, 64, 1), 0.0)
        fill_columns(dst, plane, chans, j, low, False)
        fill_columns(dst, plane, chans, j + 2, high, False)


def kernel(
    sizes,
    feats,
    w1f,
    w2f,
    w2b,
    w1b,
    cot,
    gf,
    gw1,
    gw2,
    fr,
    turn,
    x1,
    s1,
    p2r,
    x2,
    g2r,
    g2c,
    g1r,
    g1c,
    ws,
    rx,
    acc1,
    ry,
    acc2,
    rz,
    fin,
    send,
    recv,
):
    nz, ny, nx = sizes
    z, y, x, core = (lax.axis_index(a) for a in AXES)
    total = nz * ny * nx
    place = (z * ny + y) * nx + x

    def at(position, c):
        return (position // (nx * ny), (position // nx) % ny, position % nx, c)

    left = (place + total - 1) % total
    right = (place + 1) % total
    other = 1 - core
    near = [
        (z, y, x, other),
        at(left, core),
        at(left, other),
        at(right, core),
        at(right, other),
    ]
    along_x = [(z, y, (x + k) % nx, core) for k in range(1, nx)]
    along_y = [(z, (y + k) % ny, x, core) for k in range(1, ny)]
    along_z = [((z + k) % nz, y, x, core) for k in range(1, nz)]

    barrier = pltpu.get_barrier_semaphore()
    peers = near + along_x + along_y + along_z
    for peer in peers:
        pl.semaphore_signal(barrier, inc=1, device_id=peer, device_id_type=MESH)
    pl.semaphore_wait(barrier, len(peers))

    count = [0]

    def copy(src, dst, peer):
        k = count[0]
        count[0] += 1
        made = pltpu.make_async_remote_copy(
            src_ref=src,
            dst_ref=dst,
            send_sem=send.at[k],
            recv_sem=recv.at[k],
            device_id=peer,
            device_id_type=MESH,
        )
        made.start()
        return made

    started = []
    half = pl.ds(pl.multiple_of(core * 16, 16), 16)
    half2 = pl.ds(pl.multiple_of(core * 32, 32), 32)

    batch = [
        copy(feats.at[:, 0], fr.at[3, half], near[1]),
        copy(feats.at[:, 0], fr.at[3, half], near[2]),
        copy(feats.at[:, 1], fr.at[0, half], near[3]),
        copy(feats.at[:, 1], fr.at[0, half], near[4]),
        copy(feats.at[:, 0], fr.at[1, half], near[0]),
        copy(feats.at[:, 1], fr.at[2, half], near[0]),
    ]
    started += batch
    fr[1, half] = feats[:, 0]
    fr[2, half] = feats[:, 1]
    clear_rows(x1, 8)
    clear_rows(x2, 4)
    clear_rows(g2c, 4)
    clear_rows(g1c, 8)
    for c in range(32):
        turn[4, c * 8 : c * 8 + 4, 0:64] = cot[c, 0].astype(F32)
    lane = lax.broadcasted_iota(jnp.int32, (32, 128), 1)
    cots = [
        jnp.where(lane < 64, turn[4, pl.ds(r, 32, stride=8), :], 0.0) for r in range(4)
    ]
    cots = jnp.concatenate(cots, axis=1)
    lower = place > 0
    upper = place < total - 1
    for made in batch[::-1]:
        made.wait_recv()
    for p in (1, 2, 0, 3):
        turn[p] = fr[p].astype(F32).reshape(256, 128)
        for r in range(8):
            value = turn[p, pl.ds(r, 32, stride=8), :]
            if p == 0:
                value = jnp.where(lower, value, 0.0)
            if p == 3:
                value = jnp.where(upper, value, 0.0)
            fill_columns(x1, p, 32, r, value, True)

    own_w1f = w1f[half, :]
    act = []
    for plane in range(2):
        pre = jnp.dot(
            own_w1f, windows(x1, range(plane, plane + 3), 1024), preferred_element_type=F32
        )
        sig = jax.nn.sigmoid(pre)
        s1[:, plane * 1024 : (plane + 1) * 1024] = slope_of(pre, sig)
        act.append((pre * sig).astype(BF16))

    def act_row(plane, r):
        return act[plane][:, r * 128 : (r + 1) * 128]

    spots = jnp.concatenate(
        [
            jnp.concatenate(
                [act_row(a, 2 * r + b) for a in range(2) for b in range(2)], axis=1
            )
            for r in range(4)
        ],
        axis=0,
    )
    from_cell = lax.broadcasted_iota(jnp.int32, (512, 128), 0)
    to_cell = lax.broadcasted_iota(jnp.int32, (512, 128), 1)
    pool = jnp.where(((from_cell & 127) >> 1) == to_cell, 0.125, 0.0).astype(BF16)
    pooled = jnp.dot(spots, pool, preferred_element_type=F32)
    pooled = pooled.astype(BF16).astype(F32)
    p2r[1, half] = pack_rows([pooled[16 * r : 16 * r + 16] for r in range(4)]).astype(BF16)

    def exchange(ref, part):
        return [
            copy(ref.at[1, part], ref.at[2, part], near[1]),
            copy(ref.at[1, part], ref.at[2, part], near[2]),
            copy(ref.at[1, part], ref.at[0, part], near[3]),
            copy(ref.at[1, part], ref.at[0, part], near[4]),
            copy(ref.at[1, part], ref.at[1, part], near[0]),
        ]

    batch = exchange(p2r, half)
    started += batch
    for made in batch[::-1]:
        made.wait_recv()
    for p in range(3):
        packed = p2r[p].astype(F32)
        if p == 0:
            packed = jnp.where(lower, packed, 0.0)
        if p == 2:
            packed = jnp.where(upper, packed, 0.0)
        unpack_into(x2, p, 32, packed)

    pre = jnp.dot(w2f[half2, :], windows(x2, range(3), 512), preferred_element_type=F32)
    sig = jax.nn.sigmoid(pre)
    grad = cots * slope_of(pre, sig)
    grad = grad.astype(BF16).astype(F32)
    g2r[1, half2] = pack_rows([grad[:, r * 128 : (r + 1) * 128] for r in range(4)]).astype(BF16)
    batch = exchange(g2r, half2)
    started += batch
    for made in batch[::-1]:
        made.wait_recv()
    for p in range(3):
        packed = g2r[p].astype(F32)
        if p == 0:
            packed = jnp.where(lower, packed, 0.0)
        if p == 2:
            packed = jnp.where(upper, packed, 0.0)
        unpack_into(g2c, p, 64, packed)

    back = jnp.dot(w2b[half, :], windows(g2c, range(3), 512), preferred_element_type=F32)
    back = jnp.concatenate([back[:, r * 128 : (r + 1) * 128] for r in range(4)], axis=0)
    high = back.astype(BF16)
    rest = back - high.astype(F32)
    middle = rest.astype(BF16)
    low = (rest - middle.astype(F32)).astype(BF16)
    from_cell = lax.broadcasted_iota(jnp.int32, (128, 128), 0)
    to_cell = lax.broadcasted_iota(jnp.int32, (128, 128), 1)
    spread = jnp.where(from_cell == (to_cell >> 1), 1.0, 0.0).astype(BF16)
    wide = jnp.dot(
        jnp.concatenate([high, middle, low], axis=0), spread, preferred_element_type=F32
    )
    wide = (wide[0:64] + wide[64:128] + wide[128:192]) * 0.125
    for plane in range(2):
        for r in range(8):
            first = plane * 1024 + r * 128
            value = wide[(r // 2) * 16 : (r // 2) * 16 + 16] * s1[:, first : first + 128]
            g1r[1 + plane, half, r * 128 : (r + 1) * 128] = value.astype(BF16)
    both = pl.ds(1, 2)
    batch = [
        copy(g1r.at[both, half], g1r.at[both, half], near[0]),
        copy(g1r.at[1, half], g1r.at[3, half], near[1]),
        copy(g1r.at[1, half], g1r.at[3, half], near[2]),
        copy(g1r.at[2, half], g1r.at[0, half], near[3]),
        copy(g1r.at[2, half], g1r.at[0, half], near[4]),
    ]
    started += batch

    nothing = jnp.zeros((64, 512), BF16)
    contract = (((1,), (1,)), ((), ()))
    sums = lax.dot_general(
        own_windows(x2, range(3), 512, core),
        jnp.concatenate([g2c[1, 64:128, 128:640], nothing], axis=0),
        contract,
        preferred_element_type=F32,
    )

    def fill_grad(p):
        for r in range(8):
            value = g1r[p, :, r * 128 : (r + 1) * 128].astype(F32)
            if p == 0:
                value = jnp.where(lower, value, 0.0)
            if p == 3:
                value = jnp.where(upper, value, 0.0)
            fill_columns(g1c, p, 32, r, value, True)

    batch[0].wait_recv()
    fill_grad(1)
    fill_grad(2)
    for plane in range(2):
        sums += lax.dot_general(
            own_windows(x1, range(plane, plane + 3), 1024, core),
            jnp.concatenate(
                [
                    jnp.zeros((64, 1024), BF16),
                    g1c[1 + plane, 32:64, 128:1152],
                    jnp.zeros((32, 1024), BF16),
                ],
                axis=0,
            ),
            contract,
            preferred_element_type=F32,
        )
    ws[0:432] = sums
    ws[432:ROWS] = jnp.zeros((ROWS - 432, 128), F32)

    part_x = ROWS // nx
    part_y = part_x // ny

    def rows_x(i):
        return pl.ds(pl.multiple_of(i * part_x, part_x), part_x)

    def rows_y(i):
        return pl.ds(pl.multiple_of(i * part_y, part_y), part_y)

    batch_x = [copy(ws.at[rows_x(peer[2])], rx.at[x], peer) for peer in along_x]
    started += batch_x

    for made in batch[1:]:
        made.wait_recv()
    fill_grad(0)
    fill_grad(3)
    own_w1b = w1b[half, :]
    for plane in range(2):
        grad = jnp.dot(
            own_w1b, windows(g1c, range(plane, plane + 3), 1024), preferred_element_type=F32
        )
        for r in range(8):
            turn[plane, pl.ds(r, 16, stride=8), :] = grad[:, r * 128 : (r + 1) * 128]
        gf[:, plane] = turn[plane, 0:128].reshape(16, 8, 128).astype(BF16)

    for made in batch_x:
        made.wait_recv()
    sums = ws[rows_x(x)]
    for k in range(1, nx):
        sums += rx[(x + k) % nx]
    acc1[...] = sums
    batch = [copy(acc1.at[rows_y(peer[1])], ry.at[y], peer) for peer in along_y]
    started += batch
    for made in batch:
        made.wait_recv()
    sums = acc1[rows_y(y)]
    for k in range(1, ny):
        sums += ry[(y + k) % ny]
    acc2[...] = sums
    rz[z] = sums
    batch = [copy(acc2, rz.at[z], peer) for peer in along_z]
    started += batch
    for made in batch:
        made.wait_recv()
    sums = rz[0]
    for k in range(1, nz):
        sums += rz[k]
    mine = pl.ds(pl.multiple_of(x * part_x + y * part_y, part_y), part_y)
    fin[mine] = sums
    batch = [copy(fin.at[mine], fin.at[mine], peer) for peer in along_y]
    started += batch
    for made in batch:
        made.wait_recv()
    batch = [copy(fin.at[rows_x(x)], fin.at[rows_x(x)], peer) for peer in along_x]
    started += batch
    for made in batch:
        made.wait_recv()
    gw2[...] = fin[0:432, 0:64]
    gw1[...] = pltpu.roll(fin[0:432], 64, 1)[:, 0:32]
    for made in started:
        made.wait_send()


def shards(sizes, feats, weight_one, weight_two, cotangent):
    nz, ny, nx = sizes
    w1f = jnp.transpose(weight_one, (0, 2, 1)).reshape(32, 27 * 32)
    w2f = jnp.transpose(weight_two, (0, 2, 1)).reshape(64, 27 * 32)
    w2b = jnp.transpose(weight_two[:, :, ::-1], (1, 2, 0)).reshape(32, 27 * 64)
    w1b = jnp.transpose(weight_one[:, :, ::-1], (1, 2, 0)).reshape(32, 27 * 32)
    copies = 6 + 5 + 5 + 5 + 2 * (nx - 1) + 2 * (ny - 1) + (nz - 1)
    part_x = ROWS // nx
    part_y = part_x // ny
    vmem = pl.BlockSpec(memory_space=pltpu.VMEM)
    gf, gw1, gw2 = pl.pallas_call(
        functools.partial(kernel, sizes),
        out_shape=(
            jax.ShapeDtypeStruct((16, 2, 8, 128), BF16),
            jax.ShapeDtypeStruct((432, 32), F32),
            jax.ShapeDtypeStruct((432, 64), F32),
        ),
        in_specs=[vmem] * 6,
        out_specs=(vmem, vmem, vmem),
        scratch_shapes=[
            pltpu.VMEM((4, 32, 8, 128), BF16),
            pltpu.VMEM((5, 256, 128), F32),
            pltpu.VMEM((4, 96, 1280), BF16),
            pltpu.VMEM((16, 2048), F32),
            pltpu.VMEM((3, 32, 256), BF16),
            pltpu.VMEM((3, 96, 768), BF16),
            pltpu.VMEM((3, 64, 256), BF16),
            pltpu.VMEM((3, 192, 768), BF16),
            pltpu.VMEM((4, 32, 1024), BF16),
            pltpu.VMEM((4, 96, 1280), BF16),
            pltpu.VMEM((ROWS, 128), F32),
            pltpu.VMEM((nx, part_x, 128), F32),
            pltpu.VMEM((part_x, 128), F32),
            pltpu.VMEM((ny, part_y, 128), F32),
            pltpu.VMEM((part_y, 128), F32),
            pltpu.VMEM((nz, part_y, 128), F32),
            pltpu.VMEM((ROWS, 128), F32),
            pltpu.SemaphoreType.DMA((copies,)),
            pltpu.SemaphoreType.DMA((copies,)),
        ],
        compiler_params=pltpu.CompilerParams(collective_id=0, has_side_effects=True),
    )(feats, w1f, w2f, w2b, w1b, cotangent)
    gw1 = jnp.transpose(gw1.reshape(27, 16, 32), (2, 1, 0))
    gw2 = jnp.transpose(gw2.reshape(27, 16, 64), (2, 1, 0))
    return gf, gw1, gw2


def build(mesh, sizes):
    finer = Mesh(mesh.devices.reshape(*sizes, mesh.shape["chan"]), AXES)
    depth = AXES[:3]
    in_specs = (P("core", depth, None, None), P(), P(), P("core", depth, None, None))
    out_specs = (P("core", depth, None, None), P(None, "core", None), P(None, "core", None))
    return jax.shard_map(
        functools.partial(shards, sizes),
        mesh=finer,
        in_specs=in_specs,
        out_specs=out_specs,
        check_vma=False,
    )


def solution(mesh):
    return build(mesh, (8, 8, 4))
```

time: 346 us -> 71 us (0.21)
  the two profiles are of different devices: /device:TPU:1 before, /device:TPU:8 now
where the time goes in v1:
time: 71 us; the launch traced here: 70.7 us
  Pallas kernels  61.5 us (87%)
  local copies, waits for them, and re-layouts  8.5 us (12%)
    pallas_call x1, Pallas kernels, shards(): pl.pallas_call(functools.partial(kernel, sizes), out_shape=(jax.ShapeDtyp...  61.5 us
    unnamed x9, local copies, waits for them, and re-layouts  4.03 us
    reshape x1, local copies, waits for them, and re-layouts, shards(): w2f = jnp.transpose(weight_two, (0, 2, 1)).reshape(64, 27 * 32)  1.74 us

profile of v1, /device:TPU:8, one launch (start us, length us, event | category | flops | bytes accessed | tf_op | source)
XLA Modules:
  0.0 70.7 jit_solution(6928162262577950593)
XLA Ops:
  0.6 0.0 copy-start.1
  0.6 1.7 %copy.14.w2f = bf16[64,864]{1,0:T(8,128)(2,1)} copy(bf16[64,864]{0,1:T(8,128)(2,1)} %bitcast.15) | data formatting | bytes 221184 | tf_op jit(solution)/shard_map/reshape | solution.py:387
  2.4 0.0 copy-done.1
  2.4 0.0 copy-start
  2.4 0.7 %copy.15.w1b = bf16[32,864]{1,0:T(8,128)(2,1)} copy(bf16[32,864]{0,1:T(8,128)(2,1)S(1)} %bitcast.17) | data formatting | bytes 110592 | tf_op jit(solution)/shard_map/reshape | solution.py:389
  3.2 0.2 copy-done
  3.4 0.1 copy.12
  3.5 0.9 %reshape.26.w2b = bf16[32,1728]{1,0:T(8,128)(2,1)} reshape(bf16[32,27,64]{2,1,0:T(8,128)(2,1)S(1)} %copy.12) | data formatting | bytes 221184 | tf_op jit(solution)/shard_map/reshape | solution.py:388
  4.4 0.1 copy.11
  4.5 0.9 %reshape.24.w1f = bf16[32,864]{1,0:T(8,128)(2,1)} reshape(bf16[32,27,32]{2,1,0:T(8,128)(2,1)S(1)} %copy.11) | data formatting | bytes 110592 | tf_op jit(solution)/shard_map/reshape | solution.py:386
  5.3 61.5 %shard_map.67 = (bf16[16,2,8,128]{3,2,1,0:T(8,128)(2,1)}, f32[432,32]{1,0:T(8,128)}, f32[432,64]{1,0:T(8,128)}) custom-call(bf16[16,2,8,128]{3,2,1,0:T(8,128)(2,1)} %feats.1, bf16[32,864]{1,0:T(8,128)(2,1)} %reshape.24.w1f, bf16[64,864]{1,0:T(8,128)(2,1)} %copy.14.w2f, bf16[32,1728]{1,0:T(8,128)(2,1)} %reshape.26.w2b, bf16[32,864]{1,0:T(8,128)(2,1)} %copy.15.w1b, ...), custom_call_target="tpu_custom_call" | custom-call | tf_op jit(solution)/shard_map/pallas_call | solution.py:394
  66.9 1.5 %copy.19 = bf16[16,2,8,128]{3,2,1,0:T(8,128)(2,1)} copy(bf16[16,2,8,128]{3,2,1,0:T(8,128)(2,1)} %get-tuple-element.12) | data formatting | bytes 131072
  68.3 0.0 copy-start.2
  68.3 1.7 %copy.20 = f32[32,16,27]{0,1,2:T(8,128)} copy(f32[32,16,27]{0,1,2:T(8,128)} %bitcast.19) | data formatting | bytes 110592
  70.0 0.0 copy-done.2
  70.0 0.7 copy.21
  (2 shorter events, 0.0 us)
Async XLA Ops:
  0.6 1.8 %copy-start.1 = (bf16[32,32,27]{1,0,2:T(8,128)(2,1)S(1)}, bf16[32,32,27]{1,0,2:T(8,128)(2,1)}, u32[]{:S(2)}) copy-start(bf16[32,32,27]{1,0,2:T(8,128)(2,1)} %param.5) | copy-start | bytes 165892
  2.4 0.9 %copy-start = (bf16[64,32,27]{0,1,2:T(8,128)(2,1)S(1)}, bf16[64,32,27]{0,1,2:T(8,128)(2,1)}, u32[]{:S(2)}) copy-start(bf16[64,32,27]{0,1,2:T(8,128)(2,1)} %param.6) | copy-start | bytes 331780
  68.3 1.7 %copy-start.2 = (f32[432,64]{1,0:T(8,128)S(1)}, f32[432,64]{1,0:T(8,128)}, u32[]{:S(2)}) copy-start(f32[432,64]{1,0:T(8,128)} %get-tuple-element.8) | copy-start | bytes 331780

commit v2 on v1

v2 whole, which is shorter than its diff:
```python
import functools

import jax
import jax.numpy as jnp
from jax import lax
from jax.experimental import pallas as pl
from jax.experimental.pallas import tpu as pltpu
from jax.sharding import Mesh
from jax.sharding import PartitionSpec as P

MESH = pl.DeviceIdType.MESH
F32 = jnp.float32
BF16 = jnp.bfloat16
AXES = ("z", "y", "x", "core")


def slope_of(pre, sig):
    return sig * (1.0 + pre * (1.0 - sig))


def fill_columns(dst, plane, chans, row, value, edges, flip):
    lane = lax.broadcasted_iota(jnp.int32, value.shape, 1)
    before = pltpu.roll(value, 1, 1)
    after = pltpu.roll(value, 127, 1)
    if edges:
        before = jnp.where(lane == 0, 0.0, before)
        after = jnp.where(lane == 127, 0.0, after)
    where = slice((row + 1) * 128, (row + 2) * 128)
    first, last = (after, before) if flip else (before, after)
    dst[plane, 0:chans, where] = first.astype(BF16)
    dst[plane, chans : 2 * chans, where] = value.astype(BF16)
    dst[plane, 2 * chans : 3 * chans, where] = last.astype(BF16)


def clear_rows(dst, rows):
    planes, chans = dst.shape[:2]
    zero = jnp.zeros((planes, chans, 128), BF16)
    dst[:, :, 0:128] = zero
    dst[:, :, (rows + 1) * 128 : (rows + 2) * 128] = zero


def windows(src, plane, width, flip=False):
    order = (2, 1, 0) if flip else (0, 1, 2)
    return jnp.concatenate([src[plane, :, b * 128 : b * 128 + width] for b in order], axis=0)


def own_windows(src, planes, width, core):
    pieces = []
    for a in planes:
        for b in range(3):
            for c in range(3):
                first = pl.multiple_of(c * 32 + core * 16, 16)
                pieces.append(src[a, pl.ds(first, 16), b * 128 : b * 128 + width])
    return jnp.concatenate(pieces, axis=0)


def pack_rows(rows):
    return jnp.concatenate(
        [rows[0] + pltpu.roll(rows[2], 64, 1), rows[1] + pltpu.roll(rows[3], 64, 1)], axis=1
    )


def unpack_into(dst, plane, chans, packed, flip):
    lane = lax.broadcasted_iota(jnp.int32, (chans, 128), 1)
    for j in range(2):
        both = packed[:, j * 128 : (j + 1) * 128]
        low = jnp.where(lane < 64, both, 0.0)
        high = jnp.where(lane < 64, pltpu.roll(both, 64, 1), 0.0)
        fill_columns(dst, plane, chans, j, low, False, flip)
        fill_columns(dst, plane, chans, j + 2, high, False, flip)


def dot(a, b):
    return jnp.dot(a, b, preferred_element_type=F32)


def dot_rows(a, b):
    return lax.dot_general(a, b, (((1,), (1,)), ((), ())), preferred_element_type=F32)


def kernel(
    sizes,
    feats,
    weight_one,
    weight_two,
    cotangent,
    gf,
    out1,
    out2,
    w1,
    w2,
    cot,
    w1f,
    w2f,
    w2b,
    w1b,
    turned,
    fr,
    turn,
    x1,
    s1,
    p2r,
    x2,
    g2r,
    g2c,
    g1r,
    g1c,
    gfv,
    ws1,
    rx1,
    acc1,
    rz1,
    fin1,
    ws2,
    rx2,
    acc2,
    rz2,
    fin2,
    local,
    send,
    recv,
    sum_send,
    sum_recv,
):
    nz, ny, nx = sizes
    z, y, x, core = (lax.axis_index(a) for a in AXES)
    total = nz * ny * nx
    place = (z * ny + y) * nx + x
    flat = nx * ny
    half = pl.ds(pl.multiple_of(core * 16, 16), 16)
    half2 = pl.ds(pl.multiple_of(core * 32, 32), 32)

    def fetch(src, dst, k):
        made = pltpu.make_async_copy(src, dst, local.at[k])
        made.start()
        return made

    fetched = [
        fetch(feats.at[:, 0], fr.at[1, half], 0),
        fetch(feats.at[:, 1], fr.at[2, half], 1),
        fetch(weight_one, w1, 2),
        fetch(weight_two, w2, 3),
        fetch(cotangent, cot, 4),
    ]

    def at(position, c):
        return (position // (nx * ny), (position // nx) % ny, position % nx, c)

    left = (place + total - 1) % total
    right = (place + 1) % total
    other = 1 - core
    near = [
        (z, y, x, other),
        at(left, core),
        at(left, other),
        at(right, core),
        at(right, other),
    ]
    steps = [(i, j) for i in range(ny) for j in range(nx) if i or j]
    steps.sort(key=lambda s: -(min(s[0], ny - s[0]) + min(s[1], nx - s[1])))
    across = [(z, (y + i) % ny, (x + j) % nx, core) for i, j in steps]
    along_z = [((z + k) % nz, y, x, core) for k in range(1, nz)]
    mine = y * nx + x

    barrier = pltpu.get_barrier_semaphore()
    peers = near + across + along_z
    for peer in peers:
        pl.semaphore_signal(barrier, inc=1, device_id=peer, device_id_type=MESH)
    pl.semaphore_wait(barrier, len(peers))

    count = [0]
    started = []

    def copy(src, dst, peer):
        k = count[0]
        count[0] += 1
        made = pltpu.make_async_remote_copy(
            src_ref=src,
            dst_ref=dst,
            send_sem=send.at[k],
            recv_sem=recv.at[k],
            device_id=peer,
            device_id_type=MESH,
        )
        made.start()
        started.append(made)
        return made

    def spread_out(k, peers, src, dst, whole):
        for peer in peers:
            pltpu.make_async_remote_copy(
                src_ref=src(peer),
                dst_ref=dst,
                send_sem=sum_send.at[k],
                recv_sem=sum_recv.at[k],
                device_id=peer,
                device_id_type=MESH,
            ).start()
        part = whole.at[pl.ds(0, len(peers))]
        return pltpu.make_async_remote_copy(
            src_ref=part,
            dst_ref=part,
            send_sem=sum_send.at[k],
            recv_sem=sum_recv.at[k],
            device_id=peers[0],
            device_id_type=MESH,
        )

    fetched[0].wait()
    fetched[1].wait()
    own = [
        copy(fr.at[1, half], fr.at[1, half], near[0]),
        copy(fr.at[2, half], fr.at[2, half], near[0]),
    ]
    below = [copy(fr.at[2, half], fr.at[0, half], near[3]), copy(fr.at[2, half], fr.at[0, half], near[4])]
    above = [copy(fr.at[1, half], fr.at[3, half], near[1]), copy(fr.at[1, half], fr.at[3, half], near[2])]

    clear_rows(x1, 8)
    clear_rows(x2, 4)
    clear_rows(g2c, 4)
    clear_rows(g1c, 8)
    fetched[2].wait()
    for a in range(3):
        w1f[a] = jnp.concatenate(
            [w1[9 * a + t, half, :].astype(F32) for t in range(9)], axis=1
        ).astype(BF16)

    lower = place > 0
    upper = place < total - 1

    def fill_one(p):
        turn[p] = fr[p].astype(F32).reshape(256, 128)
        for r in range(8):
            value = turn[p, pl.ds(r, 32, stride=8), :]
            if p == 0:
                value = jnp.where(lower, value, 0.0)
            if p == 3:
                value = jnp.where(upper, value, 0.0)
            fill_columns(x1, p, 32, r, value, True, False)

    own[0].wait_recv()
    fill_one(1)
    own[1].wait_recv()
    fill_one(2)
    pre = [
        dot(w1f[1], windows(x1, 1, 1024)) + dot(w1f[2], windows(x1, 2, 1024)),
        dot(w1f[0], windows(x1, 1, 1024)) + dot(w1f[1], windows(x1, 2, 1024)),
    ]

    fetched[3].wait()
    for a in range(3):
        w2b[a] = jnp.concatenate(
            [w2[9 * a + t, half, :].astype(F32) for t in range(9)], axis=1
        ).astype(BF16)
        turned[0:288, 0:64] = w2[9 * a : 9 * a + 9].astype(F32).reshape(288, 64)
        for b in range(3):
            block = jnp.transpose(turned[b * 128 : (b + 1) * 128, :])
            w2f[a, :, b * 128 : (b + 1) * 128] = block[0:64].astype(BF16)
        turned[0:288, 0:32] = w1[9 * a : 9 * a + 9].astype(F32).reshape(288, 32)
        for b in range(3):
            block = jnp.transpose(turned[b * 128 : (b + 1) * 128, :])
            w1b[a, :, b * 128 : (b + 1) * 128] = block[0:32].astype(BF16)
    fetched[4].wait()
    for c in range(32):
        turn[4, c * 8 : c * 8 + 4, 0:64] = cot[c, 0].astype(F32)
    lane = lax.broadcasted_iota(jnp.int32, (32, 128), 1)
    cots = [
        jnp.where(lane < 64, turn[4, pl.ds(r, 32, stride=8), :], 0.0) for r in range(4)
    ]
    cots = jnp.concatenate(cots, axis=1)

    for made in below:
        made.wait_recv()
    fill_one(0)
    pre[0] += dot(w1f[0], windows(x1, 0, 1024))
    for made in above:
        made.wait_recv()
    fill_one(3)
    pre[1] += dot(w1f[2], windows(x1, 3, 1024))

    act = []
    for plane in range(2):
        sig = jax.nn.sigmoid(pre[plane])
        s1[:, plane * 1024 : (plane + 1) * 1024] = slope_of(pre[plane], sig)
        act.append((pre[plane] * sig).astype(BF16))

    def act_row(plane, r):
        return act[plane][:, r * 128 : (r + 1) * 128]

    spots = jnp.concatenate(
        [
            jnp.concatenate(
                [act_row(a, 2 * r + b) for a in range(2) for b in range(2)], axis=1
            )
            for r in range(4)
        ],
        axis=0,
    )
    from_cell = lax.broadcasted_iota(jnp.int32, (512, 128), 0)
    to_cell = lax.broadcasted_iota(jnp.int32, (512, 128), 1)
    pool = jnp.where(((from_cell & 127) >> 1) == to_cell, 0.125, 0.0).astype(BF16)
    pooled = dot(spots, pool).astype(BF16).astype(F32)
    p2r[1, half] = pack_rows([pooled[16 * r : 16 * r + 16] for r in range(4)]).astype(BF16)

    def exchange(ref, part):
        below = [copy(ref.at[1, part], ref.at[0, part], near[3]), copy(ref.at[1, part], ref.at[0, part], near[4])]
        above = [copy(ref.at[1, part], ref.at[2, part], near[1]), copy(ref.at[1, part], ref.at[2, part], near[2])]
        own = copy(ref.at[1, part], ref.at[1, part], near[0])
        return own, below, above

    def fill_two(src, dst, chans, p, flip):
        packed = src[p].astype(F32)
        if p == 0:
            packed = jnp.where(lower, packed, 0.0)
        if p == 2:
            packed = jnp.where(upper, packed, 0.0)
        unpack_into(dst, p, chans, packed, flip)

    own, below, above = exchange(p2r, half)
    own.wait_recv()
    fill_two(p2r, x2, 32, 1, False)

    def part_two(a):
        return dot(w2f[a, half2, 0:288], windows(x2, a, 512))

    pre = part_two(1)
    for made in below:
        made.wait_recv()
    fill_two(p2r, x2, 32, 0, False)
    pre += part_two(0)
    for made in above:
        made.wait_recv()
    fill_two(p2r, x2, 32, 2, False)
    pre += part_two(2)
    sig = jax.nn.sigmoid(pre)
    grad = (cots * slope_of(pre, sig)).astype(BF16).astype(F32)
    g2r[1, half2] = pack_rows([grad[:, r * 128 : (r + 1) * 128] for r in range(4)]).astype(BF16)

    own, below, above = exchange(g2r, half2)
    own.wait_recv()
    fill_two(g2r, g2c, 64, 1, True)

    def part_back(a):
        return dot(w2b[a], windows(g2c, 2 - a, 512, True))

    back = part_back(1)
    sums = dot_rows(
        own_windows(x2, range(3), 512, core),
        jnp.concatenate([g2c[1, 64:128, 128:640], jnp.zeros((64, 512), BF16)], axis=0),
    )
    sums = jnp.concatenate([sums, jnp.zeros((16, 128), F32)], axis=0)
    sums = sums[0:224] + pltpu.roll(sums[224:448], 64, 1)
    size2 = 256 // flat
    for i in range(flat):
        if (i + 1) * size2 <= 224:
            ws2[i] = sums[i * size2 : (i + 1) * size2]
        else:
            ws2[i] = jnp.zeros((size2, 128), F32)
            if i * size2 < 224:
                ws2[i, 0 : 224 - i * size2] = sums[i * size2 : 224]
    for made in below:
        made.wait_recv()
    fill_two(g2r, g2c, 64, 0, True)
    back += part_back(2)
    for made in above:
        made.wait_recv()
    fill_two(g2r, g2c, 64, 2, True)
    back += part_back(0)

    def chunk(ref):
        return lambda peer: ref.at[peer[1] * nx + peer[2]]

    scatter2 = spread_out(0, across, chunk(ws2), rx2.at[mine], rx2)

    back = jnp.concatenate([back[:, r * 128 : (r + 1) * 128] for r in range(4)], axis=0)
    high = back.astype(BF16)
    rest = back - high.astype(F32)
    middle = rest.astype(BF16)
    low = (rest - middle.astype(F32)).astype(BF16)
    from_cell = lax.broadcasted_iota(jnp.int32, (128, 128), 0)
    to_cell = lax.broadcasted_iota(jnp.int32, (128, 128), 1)
    repeat = jnp.where(from_cell == (to_cell >> 1), 1.0, 0.0).astype(BF16)
    wide = dot(jnp.concatenate([high, middle, low], axis=0), repeat)
    wide = (wide[0:64] + wide[64:128] + wide[128:192]) * 0.125
    for plane in range(2):
        for r in range(8):
            first = plane * 1024 + r * 128
            value = wide[(r // 2) * 16 : (r // 2) * 16 + 16] * s1[:, first : first + 128]
            g1r[1 + plane, half, r * 128 : (r + 1) * 128] = value.astype(BF16)
    both = pl.ds(1, 2)
    own = copy(g1r.at[both, half], g1r.at[both, half], near[0])
    below = [copy(g1r.at[2, half], g1r.at[0, half], near[3]), copy(g1r.at[2, half], g1r.at[0, half], near[4])]
    above = [copy(g1r.at[1, half], g1r.at[3, half], near[1]), copy(g1r.at[1, half], g1r.at[3, half], near[2])]

    own.wait_recv()
    zero = jnp.zeros((96, 1024), BF16)
    sums = dot_rows(
        own_windows(x1, range(0, 3), 1024, core), jnp.concatenate([g1r[1], zero], axis=0)
    ) + dot_rows(
        own_windows(x1, range(1, 4), 1024, core), jnp.concatenate([g1r[2], zero], axis=0)
    )
    sums = jnp.concatenate([sums, jnp.zeros((16, 128), F32)], axis=0)
    sums = (
        sums[0:112]
        + pltpu.roll(sums[112:224], 32, 1)
        + pltpu.roll(sums[224:336], 64, 1)
        + pltpu.roll(sums[336:448], 96, 1)
    )
    size1 = 128 // flat
    for i in range(flat):
        if (i + 1) * size1 <= 112:
            ws1[i] = sums[i * size1 : (i + 1) * size1]
        else:
            ws1[i] = jnp.zeros((size1, 128), F32)
            if i * size1 < 112:
                ws1[i, 0 : 112 - i * size1] = sums[i * size1 : 112]
    scatter1 = spread_out(1, across, chunk(ws1), rx1.at[mine], rx1)

    def total_of(ref, n):
        parts = [ref[k] for k in range(n)]
        while len(parts) > 1:
            parts = [a + b for a, b in zip(parts[::2], parts[1::2])]
        return parts[0]

    def to_z(k, scatter, ws, rx, acc, rz):
        rx[mine] = ws[mine]
        scatter.wait_recv()
        part = total_of(rx, flat)
        acc[...] = part
        rz[z] = part
        return spread_out(k, along_z, lambda peer: acc, rz.at[z], rz)

    def to_all(k, meet, rz, fin):
        meet.wait_recv()
        fin[mine] = total_of(rz, nz)
        return spread_out(k, across, lambda peer: fin.at[mine], fin.at[mine], fin)

    meet2 = to_z(2, scatter2, ws2, rx2, acc2, rz2)

    def fill_grad(p):
        for r in range(8):
            value = g1r[p, :, r * 128 : (r + 1) * 128].astype(F32)
            if p == 0:
                value = jnp.where(lower, value, 0.0)
            if p == 3:
                value = jnp.where(upper, value, 0.0)
            fill_columns(g1c, p, 32, r, value, True, True)

    fill_grad(1)
    fill_grad(2)
    for made in below + above:
        made.wait_recv()
    fill_grad(0)
    fill_grad(3)
    for plane in range(2):
        grad = sum(
            dot(w1b[a, half, 0:288], windows(g1c, plane + 2 - a, 1024, True)) for a in range(3)
        )
        for r in range(8):
            turn[plane, pl.ds(r, 16, stride=8), :] = grad[:, r * 128 : (r + 1) * 128]
        gfv[:, plane] = turn[plane, 0:128].reshape(16, 8, 128).astype(BF16)
    stored = fetch(gfv, gf, 5)

    meet1 = to_z(3, scatter1, ws1, rx1, acc1, rz1)
    gather2 = to_all(4, meet2, rz2, fin2)
    gather1 = to_all(5, meet1, rz1, fin1)
    for made in started:
        made.wait_send()
    for made in (scatter1, scatter2, meet1, meet2):
        made.wait_send()
    stored.wait()
    gather2.wait()
    out2[...] = fin2[...]
    gather1.wait()
    out1[...] = fin1[...]


def finish(flat, gf, sum1, sum2, gf_out, gw1, gw2, all1, all2):
    gf_out[...] = gf[...]
    size1, size2 = 128 // flat, 256 // flat
    for i in range(flat):
        all1[i * size1 : (i + 1) * size1] = sum1[i]
        all2[i * size2 : (i + 1) * size2] = sum2[i]
    for j in range(4):
        rows = min(112, 432 - j * 112)
        part = all1[0:rows]
        part = pltpu.roll(part, 128 - 32 * j, 1) if j else part
        gw1[j * 112 : j * 112 + rows] = part[:, 0:32]
    gw2[0:224] = all2[0:224, 0:64]
    gw2[224:432] = pltpu.roll(all2[0:208], 64, 1)[:, 0:64]


def shards(sizes, feats, weight_one, weight_two, cotangent):
    nz, ny, nx = sizes
    flat = nx * ny
    w1 = jnp.transpose(weight_one, (2, 0, 1))
    w2 = jnp.transpose(weight_two, (2, 1, 0))
    vmem = pl.BlockSpec(memory_space=pltpu.VMEM)
    anywhere = pl.BlockSpec(memory_space=pl.ANY)
    copies = 6 + 5 + 5 + 5

    def scratch(rows):
        return [
            pltpu.VMEM((flat, rows // flat, 128), F32),
            pltpu.VMEM((flat, rows // flat, 128), F32),
            pltpu.VMEM((rows // flat, 128), F32),
            pltpu.VMEM((nz, rows // flat, 128), F32),
            pltpu.VMEM((flat, rows // flat, 128), F32),
        ]

    gf, sum1, sum2 = pl.pallas_call(
        functools.partial(kernel, sizes),
        out_shape=(
            jax.ShapeDtypeStruct((16, 2, 8, 128), BF16),
            jax.ShapeDtypeStruct((flat, 128 // flat, 128), F32),
            jax.ShapeDtypeStruct((flat, 256 // flat, 128), F32),
        ),
        in_specs=[anywhere] * 4,
        out_specs=(anywhere, vmem, vmem),
        scratch_shapes=[
            pltpu.VMEM((27, 32, 32), BF16),
            pltpu.VMEM((27, 32, 64), BF16),
            pltpu.VMEM((32, 1, 4, 64), BF16),
            pltpu.VMEM((3, 16, 288), BF16),
            pltpu.VMEM((3, 64, 384), BF16),
            pltpu.VMEM((3, 16, 576), BF16),
            pltpu.VMEM((3, 32, 384), BF16),
            pltpu.VMEM((384, 128), F32),
            pltpu.VMEM((4, 32, 8, 128), BF16),
            pltpu.VMEM((5, 256, 128), F32),
            pltpu.VMEM((4, 96, 1280), BF16),
            pltpu.VMEM((16, 2048), F32),
            pltpu.VMEM((3, 32, 256), BF16),
            pltpu.VMEM((3, 96, 768), BF16),
            pltpu.VMEM((3, 64, 256), BF16),
            pltpu.VMEM((3, 192, 768), BF16),
            pltpu.VMEM((4, 32, 1024), BF16),
            pltpu.VMEM((4, 96, 1280), BF16),
            pltpu.VMEM((16, 2, 8, 128), BF16),
            *scratch(128),
            *scratch(256),
            pltpu.SemaphoreType.DMA((6,)),
            pltpu.SemaphoreType.DMA((copies,)),
            pltpu.SemaphoreType.DMA((copies,)),
            pltpu.SemaphoreType.DMA((6,)),
            pltpu.SemaphoreType.DMA((6,)),
        ],
        compiler_params=pltpu.CompilerParams(
            collective_id=0, has_side_effects=True, vmem_limit_bytes=32 * 2**20
        ),
    )(feats, w1, w2, cotangent)
    gf, gw1, gw2 = pl.pallas_call(
        functools.partial(finish, flat),
        out_shape=(
            jax.ShapeDtypeStruct((16, 2, 8, 128), BF16),
            jax.ShapeDtypeStruct((432, 32), F32),
            jax.ShapeDtypeStruct((432, 64), F32),
        ),
        in_specs=[vmem] * 3,
        out_specs=(vmem, vmem, vmem),
        scratch_shapes=[pltpu.VMEM((128, 128), F32), pltpu.VMEM((256, 128), F32)],
        compiler_params=pltpu.CompilerParams(vmem_limit_bytes=8 * 2**20),
    )(gf, sum1, sum2)
    gw1 = jnp.transpose(gw1.reshape(27, 16, 32), (2, 1, 0))
    gw2 = jnp.transpose(gw2.reshape(27, 16, 64), (2, 1, 0))
    return gf, gw1, gw2


def build(mesh, sizes):
    finer = Mesh(mesh.devices.reshape(*sizes, mesh.shape["chan"]), AXES)
    depth = AXES[:3]
    in_specs = (P("core", depth, None, None), P(), P(), P("core", depth, None, None))
    out_specs = (P("core", depth, None, None), P(None, "core", None), P(None, "core", None))
    return jax.shard_map(
        functools.partial(shards, sizes),
        mesh=finer,
        in_specs=in_specs,
        out_specs=out_specs,
        check_vma=False,
    )


def solution(mesh):
    return build(mesh, (8, 8, 4))
```

time: 71 us -> 57.4 us (0.81)
  the two profiles are of different devices: /device:TPU:8 before, /device:TPU:1 now
where the time goes in v2:
time: 57.4 us; the launch traced here: 56.9 us
  Pallas kernels  52.8 us (92%)
  local copies, waits for them, and re-layouts  3.46 us (6%)
  between operations  0.65 us (1%)
    pallas_call x1, Pallas kernels, shards(): pl.pallas_call(functools.partial(kernel, sizes), out_shape=(jax.ShapeDtyp...  51.9 us
    unnamed x8, local copies, waits for them, and re-layouts  3.46 us

profile of v2, /device:TPU:1, one launch (start us, length us, event | category | flops | bytes accessed | tf_op | source)
XLA Modules:
  0.0 56.9 jit_solution(12795669444968284705)
XLA Ops:
  0.6 0.0 copy-start
  0.6 0.9 %copy-done = bf16[32,32,27]{1,0,2:T(8,128)(2,1)S(1)} copy-done((bf16[32,32,27]{1,0,2:T(8,128)(2,1)S(1)}, bf16[32,32,27]{1,0,2:T(8,128)(2,1)}, u32[]{:S(2)}) %copy-start) | copy-done | bytes 55320
  1.6 0.0 copy-start.1
  1.6 0.9 %copy-done.1 = bf16[64,32,27]{0,1,2:T(8,128)(2,1)S(1)} copy-done((bf16[64,32,27]{0,1,2:T(8,128)(2,1)S(1)}, bf16[64,32,27]{0,1,2:T(8,128)(2,1)}, u32[]{:S(2)}) %copy-start.1) | copy-done | bytes 110616
  2.5 0.0 copy-start.2
  2.5 0.8 %copy-done.2 = bf16[16,2,8,128]{3,2,1,0:T(8,128)(2,1)S(1)} copy-done((bf16[16,2,8,128]{3,2,1,0:T(8,128)(2,1)S(1)}, bf16[16,2,8,128]{3,2,1,0:T(8,128)(2,1)}, u32[]{:S(2)}) %copy-start.2) | copy-done | bytes 65560
  3.3 0.0 copy-start.3
  3.3 0.8 %copy-done.3 = bf16[32,1,4,64]{3,2,1,0:T(4,128)(2,1)S(1)} copy-done((bf16[32,1,4,64]{3,2,1,0:T(4,128)(2,1)S(1)}, bf16[32,1,4,64]{3,2,1,0:T(4,128)(2,1)}, u32[]{:S(2)}) %copy-start.3) | copy-done | bytes 16408
  4.1 51.9 %shard_map.67 = (bf16[16,2,8,128]{3,2,1,0:T(8,128)(2,1)S(1)}, f32[32,4,128]{2,1,0:T(4,128)S(1)}, f32[32,8,128]{2,1,0:T(8,128)S(1)}) custom-call(bf16[16,2,8,128]{3,2,1,0:T(8,128)(2,1)S(1)} %copy-done.2, bf16[27,32,32]{2,1,0:T(8,128)(2,1)S(1)} %bitcast.8, bf16[27,32,64]{2,1,0:T(8,128)(2,1)S(1)} %bitcast.9, bf16[32,1,4,64]{3,2,1,0:T(4,128)(2,1)S(1)} %copy-done.3), custom_call_target="tpu_custom_call" | custom-call | tf_op jit(solution)/shard_map/pallas_call | solution.py:511
  56.0 0.9 %shard_map.68 = (bf16[16,2,8,128]{3,2,1,0:T(8,128)(2,1)}, f32[432,32]{1,0:T(8,128)}, f32[432,64]{1,0:T(8,128)}) custom-call(bf16[16,2,8,128]{3,2,1,0:T(8,128)(2,1)S(1)} %get-tuple-element.9.gf, f32[32,4,128]{2,1,0:T(4,128)S(1)} %get-tuple-element.10.sum1, f32[32,8,128]{2,1,0:T(8,128)S(1)} %get-tuple-element.11.sum2), custom_call_target="tpu_custom_call" | custom-call | tf_op jit(solution)/shard_map/pallas_call | solution.py:552
Async XLA Ops:
  0.6 0.9 %copy-start = (bf16[32,32,27]{1,0,2:T(8,128)(2,1)S(1)}, bf16[32,32,27]{1,0,2:T(8,128)(2,1)}, u32[]{:S(2)}) copy-start(bf16[32,32,27]{1,0,2:T(8,128)(2,1)} %param.5) | copy-start | bytes 165892
  1.6 0.9 %copy-start.1 = (bf16[64,32,27]{0,1,2:T(8,128)(2,1)S(1)}, bf16[64,32,27]{0,1,2:T(8,128)(2,1)}, u32[]{:S(2)}) copy-start(bf16[64,32,27]{0,1,2:T(8,128)(2,1)} %param.6) | copy-start | bytes 331780
  2.5 0.8 %copy-start.2 = (bf16[16,2,8,128]{3,2,1,0:T(8,128)(2,1)S(1)}, bf16[16,2,8,128]{3,2,1,0:T(8,128)(2,1)}, u32[]{:S(2)}) copy-start(bf16[16,2,8,128]{3,2,1,0:T(8,128)(2,1)} %feats.1) | copy-start | bytes 196612
  3.3 0.8 %copy-start.3 = (bf16[32,1,4,64]{3,2,1,0:T(4,128)(2,1)S(1)}, bf16[32,1,4,64]{3,2,1,0:T(4,128)(2,1)}, u32[]{:S(2)}) copy-start(bf16[32,1,4,64]{3,2,1,0:T(4,128)(2,1)} %cotangent.1) | copy-start | bytes 49156
